TPU v7x, 512 devices: a whole 4x8x8 slice. The times are simulated.
512 devices in a mesh: band: 32 (over y_lo, x, core), plane: 16 (over y_hi, z).
Axes of the slice: x: 4, y: 8 (y_hi: 2, y_lo: 4; y = y_hi * 4 + y_lo), z: 8, core: 2. Of those that a mesh axis runs over, the one named last changes fastest.
Arguments:
- orbitals: bfloat16 [64, 128, 128, 128], P('band', 'plane'), may hold values from -6 to 6
- potential_slots: bfloat16 [32, 2, 128, 128, 128], P('band', None, 'plane'), may hold values from -6 to 6
- pattern_owner: int32 [4], replicated, may hold values from 0 to 31, as said below
- retained: int32 [3, 64], replicated, may hold values from 0 to 127, as said below
- band_energy: float32 [64], P('band'), may hold values from 0.5 to 8
Outputs:
- rhs: float32 [64, 4, 64, 64, 128], P('band', None, None, 'plane')
Inputs may be any that keep to these rules, and one draw needn't show every extreme that they name: pattern_owner holds 4 distinct slot indices. Each row of retained holds 64 distinct frequency indices.
All inputs are finite; a program needn't handle non-finite values.
Results may differ from a plain program's by a relative error of at most 0.0003.
Values may be sent and summed in bfloat16 or wider, within the bound.
A program may use at most 64 MiB of HBM per device.

v0:
```python
import math

import jax
import jax.numpy as jnp
from jax import lax
from jax.sharding import PartitionSpec as P

kinetic_coef = 0.5 * (2.0 * math.pi / 64.0) ** 2


def broadcast(block, axis, holder):
    block = jnp.where(lax.axis_index(axis) == holder, block, jnp.zeros_like(block))
    return lax.psum(block, axis)


def make_table(frequency, length):
    position = jnp.arange(length, dtype=jnp.int32)
    phase_index = position[:, None] * frequency[None, :] % length
    angles = phase_index.astype(jnp.float32) * (2.0 * math.pi / length)
    norm_factor = 1.0 / math.sqrt(length)
    return jnp.concatenate([jnp.cos(angles), -jnp.sin(angles)], axis=1) * norm_factor


def signed_square(frequency, length):
    signed = jnp.where(frequency < length // 2, frequency, frequency - length).astype(jnp.float32)
    return signed * signed


def fetch_potential(potential_slots, slot_index):
    return broadcast(potential_slots, "band", slot_index)


def per_device(orbitals, potential_slots, pattern_owner, retained, band_energy):
    length = orbitals.shape[2]
    kept_count = retained.shape[1]
    highest = lax.Precision.HIGHEST
    table_x = make_table(retained[0], length)
    table_y = make_table(retained[1], length)
    table_z = make_table(retained[2], length)
    plane_rank = lax.axis_index("plane")
    plane_count = lax.axis_size("plane")
    local_keep = kept_count // plane_count
    ky_local = lax.dynamic_slice_in_dim(retained[1], plane_rank * local_keep, local_keep)
    kinetic = kinetic_coef * (
        signed_square(retained[0], length)[:, None, None]
        + signed_square(ky_local, length)[None, :, None]
        + signed_square(retained[2], length)[None, None, :]
    )
    precond = 1.0 / (1.0 + kinetic[None] / band_energy[:, None, None, None])
    results = []
    for pattern in range(pattern_owner.shape[0]):
        potential = fetch_potential(potential_slots, pattern_owner[pattern])
        planar_potential = potential[0]
        product = orbitals[None].astype(jnp.float32) * planar_potential[:, None].astype(jnp.float32)
        along_z = jnp.dot(product.reshape(-1, length), table_z, precision=highest).reshape(
            product.shape[:-1] + (2 * kept_count,)
        )
        mixed_z = jnp.concatenate(
            [
                along_z[0, ..., :kept_count] - along_z[1, ..., kept_count:],
                along_z[0, ..., kept_count:] + along_z[1, ..., :kept_count],
            ],
            axis=-1,
        )
        along_y = jnp.einsum("yj,bxyc->bxjc", table_y, mixed_z, precision=highest)
        planes = jnp.concatenate(
            [
                along_y[:, :, :kept_count, :kept_count] - along_y[:, :, kept_count:, kept_count:],
                along_y[:, :, kept_count:, :kept_count] + along_y[:, :, :kept_count, kept_count:],
            ],
            axis=-1,
        )[:, None]
        along_x = jnp.einsum(
            "xi,bpxjc->bpijc",
            table_x,
            lax.all_to_all(planes, "plane", split_axis=3, concat_axis=2, tiled=True),
            precision=highest,
        )
        real_part = (
            along_x[:, :, :kept_count, :, :kept_count] - along_x[:, :, kept_count:, :, kept_count:]
        )
        imag_part = (
            along_x[:, :, kept_count:, :, :kept_count] + along_x[:, :, :kept_count, :, kept_count:]
        )
        results.append(
            jnp.concatenate([real_part * precond[:, None], imag_part * precond[:, None]], axis=-1)
        )
    return jnp.concatenate(results, axis=1)


def solution(mesh):
    in_specs = (
        P("band", "plane", None, None),
        P("band", None, "plane", None, None),
        P(),
        P(),
        P("band"),
    )
    out_specs = P("band", None, None, "plane", None)
    return jax.shard_map(
        per_device, mesh=mesh, in_specs=in_specs, out_specs=out_specs, check_vma=False
    )
```

profile of v0, /device:TPU:1, one launch (start us, length us, event | category | flops | bytes accessed | tf_op | source)
XLA Modules:
  0.0 420.4 jit_solution(9479548974322862593)
XLA Ops:
  6.5 1.5 fusion.120
  10.5 2.5 select_bitcast_fusion.3
  14.2 293.0 %all-reduce.3.cloned.1.call-done = (bf16[2,8,128,128]{3,2,1,0:T(8,128)(2,1)}, bf16[2,8,128,128]{3,2,1,0:T(8,128)(2,1)}, bf16[2,8,128,128]{3,2,1,0:T(8,128)(2,1)}, bf16[2,8,128,128]{3,2,1,0:T(8,128)(2,1)}) async-done(((bf16[2,8,128,128]{3,2,1,0:T(8,128)(2,1)}, bf16[2,8,128,128]{3,2,1,0:T(8,128)(2,1)}, bf16[2,8,128,128]{3,2,1,0:T(8,128)(2,1)}, bf16[2,8,128,128]{3,2,1,0:T(8,128)(2,1)}), ...) | async-done | bytes 2097168 | tf_op jit(solution)/shard_map/psum | solution.py:13
  307.2 1.1 convert_element_type.95
  308.3 2.2 fusion
  312.3 1.1 copy.25
  313.4 10.1 %all-to-all-start.3 = ((f32[2,1,8,64,128]{4,2,0,1,3:T(8,128)}), f32[2,1,8,64,128]{4,2,0,1,3:T(8,128)S(1)}, u32[]{:S(2)}, u32[]{:S(2)}) async-start(f32[2,1,8,64,128]{4,2,0,1,3:T(8,128)} %copy.25), calls=%async_computation.3 | async-start | bytes 1048576 | tf_op jit(solution)/shard_map/all_to_all | solution.py:76
  323.7 2.2 fusion.2
  327.7 1.1 copy.22
  328.9 8.3 %all-to-all-done.3 = f32[2,1,8,64,128]{4,2,0,1,3:T(8,128)S(1)} async-done(((f32[2,1,8,64,128]{4,2,0,1,3:T(8,128)}), f32[2,1,8,64,128]{4,2,0,1,3:T(8,128)S(1)}, u32[]{:S(2)}, u32[]{:S(2)}) %all-to-all-start.3) | async-done | bytes 524320 | tf_op jit(solution)/shard_map/all_to_all | solution.py:76
  337.1 9.4 %all-to-all-start.2 = ((f32[2,1,8,64,128]{4,2,0,1,3:T(8,128)}), f32[2,1,8,64,128]{4,2,0,1,3:T(8,128)S(1)}, u32[]{:S(2)}, u32[]{:S(2)}) async-start(f32[2,1,8,64,128]{4,2,0,1,3:T(8,128)} %copy.22), calls=%async_computation.2 | async-start | bytes 1048576 | tf_op jit(solution)/shard_map/all_to_all | solution.py:76
  346.5 2.1 fusion.4
  348.9 1.1 convolution_bitcast_fusion.2
  350.5 1.1 copy.19
  351.7 8.8 %all-to-all-done.2 = f32[2,1,8,64,128]{4,2,0,1,3:T(8,128)S(1)} async-done(((f32[2,1,8,64,128]{4,2,0,1,3:T(8,128)}), f32[2,1,8,64,128]{4,2,0,1,3:T(8,128)S(1)}, u32[]{:S(2)}, u32[]{:S(2)}) %all-to-all-start.2) | async-done | bytes 524320 | tf_op jit(solution)/shard_map/all_to_all | solution.py:76
  360.5 10.3 %all-to-all-start.1 = ((f32[2,1,8,64,128]{4,2,0,1,3:T(8,128)}), f32[2,1,8,64,128]{4,2,0,1,3:T(8,128)}, u32[]{:S(2)}, u32[]{:S(2)}) async-start(f32[2,1,8,64,128]{4,2,0,1,3:T(8,128)} %copy.19), calls=%async_computation.1 | async-start | bytes 1048576 | tf_op jit(solution)/shard_map/all_to_all | solution.py:76
  370.9 2.1 fusion.6
  373.2 1.1 convolution_bitcast_fusion.3
  374.9 1.1 copy.16
  376.0 9.7 %all-to-all-done.1 = f32[2,1,8,64,128]{4,2,0,1,3:T(8,128)} async-done(((f32[2,1,8,64,128]{4,2,0,1,3:T(8,128)}), f32[2,1,8,64,128]{4,2,0,1,3:T(8,128)}, u32[]{:S(2)}, u32[]{:S(2)}) %all-to-all-start.1) | async-done | bytes 524320 | tf_op jit(solution)/shard_map/all_to_all | solution.py:76
  385.7 9.9 %all-to-all-start = ((f32[2,1,8,64,128]{4,2,0,1,3:T(8,128)}), f32[2,1,8,64,128]{4,2,0,1,3:T(8,128)S(1)}, u32[]{:S(2)}, u32[]{:S(2)}) async-start(f32[2,1,8,64,128]{4,2,0,1,3:T(8,128)} %copy.16), calls=%async_computation | async-start | bytes 1048576 | tf_op jit(solution)/shard_map/all_to_all | solution.py:76
  397.2 1.6 convolution_bitcast_fusion.6
  398.9 11.5 %all-to-all-done = f32[2,1,8,64,128]{4,2,0,1,3:T(8,128)S(1)} async-done(((f32[2,1,8,64,128]{4,2,0,1,3:T(8,128)}), f32[2,1,8,64,128]{4,2,0,1,3:T(8,128)S(1)}, u32[]{:S(2)}, u32[]{:S(2)}) %all-to-all-start) | async-done | bytes 524320 | tf_op jit(solution)/shard_map/all_to_all | solution.py:76
  411.9 1.6 copy.27
  (45 shorter events, 9.6 us)
Async XLA Ops:
  6.5 300.6 %all-reduce.3.cloned.1.call-start = ((), (), s32[]{:S(2)}) async-start(), calls=%async_computation.4 | async-start | bytes 4194304 | tf_op jit(solution)/shard_map/psum | solution.py:13
  10.5 2.5 copy-start
  12.9 0.7 copy-start.4
  312.1 11.4 %copy-start.3 = (bf16[2,8,128,128]{3,2,1,0:T(8,128)(2,1)S(1)}, bf16[2,8,128,128]{3,2,1,0:T(8,128)(2,1)}, u32[]{:S(2)}) copy-start(bf16[2,8,128,128]{3,2,1,0:T(8,128)(2,1)} %get-tuple-element.6) | copy-start | bytes 1572868
  313.4 23.7 %all-to-all-start.3 = ((f32[2,1,8,64,128]{4,2,0,1,3:T(8,128)}), f32[2,1,8,64,128]{4,2,0,1,3:T(8,128)S(1)}, u32[]{:S(2)}, u32[]{:S(2)}) async-start(f32[2,1,8,64,128]{4,2,0,1,3:T(8,128)} %copy.25), calls=%async_computation.3 | async-start | bytes 1048576 | tf_op jit(solution)/shard_map/all_to_all | solution.py:76
  327.4 1.3 copy-start.2
  337.1 23.4 %all-to-all-start.2 = ((f32[2,1,8,64,128]{4,2,0,1,3:T(8,128)}), f32[2,1,8,64,128]{4,2,0,1,3:T(8,128)S(1)}, u32[]{:S(2)}, u32[]{:S(2)}) async-start(f32[2,1,8,64,128]{4,2,0,1,3:T(8,128)} %copy.22), calls=%async_computation.2 | async-start | bytes 1048576 | tf_op jit(solution)/shard_map/all_to_all | solution.py:76
  350.3 1.3 copy-start.1
  360.5 25.1 %all-to-all-start.1 = ((f32[2,1,8,64,128]{4,2,0,1,3:T(8,128)}), f32[2,1,8,64,128]{4,2,0,1,3:T(8,128)}, u32[]{:S(2)}, u32[]{:S(2)}) async-start(f32[2,1,8,64,128]{4,2,0,1,3:T(8,128)} %copy.19), calls=%async_computation.1 | async-start | bytes 1048576 | tf_op jit(solution)/shard_map/all_to_all | solution.py:76
  385.7 24.7 %all-to-all-start = ((f32[2,1,8,64,128]{4,2,0,1,3:T(8,128)}), f32[2,1,8,64,128]{4,2,0,1,3:T(8,128)S(1)}, u32[]{:S(2)}, u32[]{:S(2)}) async-start(f32[2,1,8,64,128]{4,2,0,1,3:T(8,128)} %copy.16), calls=%async_computation | async-start | bytes 1048576 | tf_op jit(solution)/shard_map/all_to_all | solution.py:76
  396.0 15.0 %copy-start.5 = (f32[2]{0:T(128)S(1)}, f32[2]{0:T(128)}, u32[]{:S(2)}) copy-start(f32[2]{0:T(128)} %param.9) | copy-start | bytes 28
Sparse Core Ops, SparseCore 0:
  13.1 294.0 all-reduce.2
where the time goes:
time: 422 us; the launch traced here: 420 us
  waiting for transfers between devices  331 us (78%)
  starting transfers between devices  39.8 us (9%)
  matrix products  16.4 us (4%)
  between operations  16.2 us (4%)
  other arithmetic  8.69 us (2%)
  local copies, waits for them, and re-layouts  8.1 us (2%)
    psum x1, waiting for transfers between devices, broadcast(): return lax.psum(block, axis)  293 us
    all_to_all x4, starting transfers between devices, per_device(): lax.all_to_all(planes, 'plane', split_axis=3, concat_axis=2, tiled=True)  39.8 us
    all_to_all x4, waiting for transfers between devices, per_device(): lax.all_to_all(planes, 'plane', split_axis=3, concat_axis=2, tiled=True)  38.2 us
    dot_general x4, matrix products, per_device(): jnp.dot(product.reshape(-1, length), table_z, precision=highest)  8.63 us
  transfers between devices with their start and end apart: 5, of which 5 were waited for; matrix products, arithmetic and copies ran while one was open for 5% of the time, Pallas kernels for 0%

commit v1 on v0

v1 whole, which is shorter than its diff:
```python
import functools
import math

import jax
import jax.numpy as jnp
from jax import lax
from jax.experimental import pallas as pl
from jax.experimental.pallas import tpu as pltpu
from jax.sharding import PartitionSpec as P

kinetic_coef = 0.5 * (2.0 * math.pi / 64.0) ** 2
MESH = pl.DeviceIdType.MESH
F32 = jnp.float32
BF16 = jnp.bfloat16
PAD = 72
POWER = 17.5
RANGE = 8192.0
SHIFT = 125.0 * math.log(2.0)


def make_table(frequency, length):
    position = jnp.arange(length, dtype=jnp.int32)
    phase_index = position[:, None] * frequency[None, :] % length
    angles = phase_index.astype(F32) * (2.0 * math.pi / length)
    norm_factor = 1.0 / math.sqrt(length)
    return jnp.cos(angles) * norm_factor, -jnp.sin(angles) * norm_factor


def signed_square(frequency, length):
    signed = jnp.where(frequency < length // 2, frequency, frequency - length).astype(F32)
    return signed * signed


def split(table):
    high = lax.reduce_precision(table, 8, 7)
    return high.astype(BF16), (table - high).astype(BF16)


def encode(value, inverse_scale):
    u = jnp.abs(value) * inverse_scale
    w = u + jnp.sqrt(u * u + 1.0)
    code = jnp.exp(POWER * jnp.log(w) - SHIFT)
    return jnp.where(value < 0.0, -code, code).astype(BF16)


def decode(code, scale):
    code = code.astype(F32)
    w = jnp.exp((jnp.log(jnp.abs(code)) + SHIFT) * (1.0 / POWER))
    u = (0.5 * scale) * (w - 1.0 / w)
    return jnp.where(code < 0.0, -u, u)


def parts(value):
    high = value.astype(BF16)
    return high, (value - high.astype(F32)).astype(BF16)


def dot(a, b):
    return jnp.dot(a, b, preferred_element_type=F32)


def kernel(
    owner, energy, ky2, orb, slot, wz, wy, wx, kx2, kz2, out,
    chunks, pot, cols, sent, got, scale_out, scale_in,
    a_send, a_recv, y_send, y_recv, x_send, x_recv, c_send, c_recv,
    d_send, d_recv, s_send, s_recv,
):
    band, plane = lax.axis_index("band"), lax.axis_index("plane")
    row, spot = band // 8, band % 8
    col, core = spot // 2, spot % 2
    n_pat = 4

    barrier = pltpu.get_barrier_semaphore()

    def greet_band(o, _):
        pl.semaphore_signal(barrier, 1, device_id={"band": (band + o) % 32}, device_id_type=MESH)
        return 0

    def greet_plane(o, _):
        pl.semaphore_signal(barrier, 1, device_id={"plane": (plane + o) % 16}, device_id_type=MESH)
        return 0

    lax.fori_loop(1, 32, greet_band, 0)
    lax.fori_loop(1, 16, greet_plane, 0)
    pl.semaphore_wait(barrier, 46)

    def chunk_copy(o):
        peer = (band + o) % 32
        return pltpu.make_async_remote_copy(
            src_ref=slot.at[:, peer % 8, pl.ds(pl.multiple_of(32 * (peer // 8), 32), 32), :],
            dst_ref=chunks.at[band],
            send_sem=a_send.at[o], recv_sem=a_recv.at[o],
            device_id={"band": peer}, device_id_type=MESH,
        )

    def chunk_arrival(o):
        src = (band - o + 32) % 32
        return pltpu.make_async_remote_copy(
            src_ref=chunks.at[src], dst_ref=chunks.at[src],
            send_sem=a_send.at[o], recv_sem=a_recv.at[o],
            device_id={"band": src}, device_id_type=MESH,
        )

    def loop(lo, hi, f):
        def body(o, _):
            f(o)
            return 0
        lax.fori_loop(lo, hi, body, 0)

    loop(1, 32, lambda o: chunk_copy(o).start())
    chunks[band] = slot[:, spot, pl.ds(pl.multiple_of(32 * row, 32), 32), :]
    loop(1, 32, lambda o: chunk_arrival(o).wait_recv())

    def y_copy(p, o):
        return pltpu.make_async_remote_copy(
            src_ref=pot.at[p, spot, row], dst_ref=pot.at[p, spot, row],
            send_sem=y_send.at[p, o], recv_sem=y_recv.at[p, o],
            device_id={"band": (row + o) % 4 * 8 + spot}, device_id_type=MESH,
        )

    def y_arrival(p, o):
        src = (row - o + 4) % 4
        return pltpu.make_async_remote_copy(
            src_ref=pot.at[p, spot, src], dst_ref=pot.at[p, spot, src],
            send_sem=y_send.at[p, o], recv_sem=y_recv.at[p, o],
            device_id={"band": src * 8 + spot}, device_id_type=MESH,
        )

    def x_copy(p, o):
        return pltpu.make_async_remote_copy(
            src_ref=pot.at[p, spot], dst_ref=pot.at[p, spot],
            send_sem=x_send.at[p, o], recv_sem=x_recv.at[p, o],
            device_id={"band": row * 8 + (col + o) % 4 * 2 + core}, device_id_type=MESH,
        )

    def x_arrival(p, o):
        src = (col - o + 4) % 4 * 2 + core
        return pltpu.make_async_remote_copy(
            src_ref=pot.at[p, src], dst_ref=pot.at[p, src],
            send_sem=x_send.at[p, o], recv_sem=x_recv.at[p, o],
            device_id={"band": row * 8 + src}, device_id_type=MESH,
        )

    def core_copy(p, o):
        src = (col - o + 4) % 4 * 2 + core
        return pltpu.make_async_remote_copy(
            src_ref=pot.at[p, src], dst_ref=pot.at[p, src],
            send_sem=c_send.at[p, o], recv_sem=c_recv.at[p, o],
            device_id={"band": row * 8 + col * 2 + 1 - core}, device_id_type=MESH,
        )

    def core_arrival(p, o):
        src = (col - o + 4) % 4 * 2 + 1 - core
        return pltpu.make_async_remote_copy(
            src_ref=pot.at[p, src], dst_ref=pot.at[p, src],
            send_sem=c_send.at[p, o], recv_sem=c_recv.at[p, o],
            device_id={"band": row * 8 + col * 2 + 1 - core}, device_id_type=MESH,
        )

    for p in range(n_pat):
        pot[p, spot, row] = chunks[owner[p]]
        loop(1, 4, lambda o: y_copy(p, o).start())

    def spread(p, _):
        loop(1, 4, lambda o: y_arrival(p, o).wait_recv())
        loop(1, 4, lambda o: x_copy(p, o).start())
        core_copy(p, 0).start()
        return 0

    lax.fori_loop(0, n_pat, spread, 0)

    def col_copy(p, o):
        peer = (plane + o) % 16
        return pltpu.make_async_remote_copy(
            src_ref=sent.at[p, peer], dst_ref=got.at[p, plane],
            send_sem=d_send.at[p, o], recv_sem=d_recv.at[p, o],
            device_id={"plane": peer}, device_id_type=MESH,
        )

    def col_arrival(p, o):
        src = (plane - o + 16) % 16
        return pltpu.make_async_remote_copy(
            src_ref=got.at[p, src], dst_ref=got.at[p, src],
            send_sem=d_send.at[p, o], recv_sem=d_recv.at[p, o],
            device_id={"plane": src}, device_id_type=MESH,
        )

    def scale_copy(p, o):
        return pltpu.make_async_remote_copy(
            src_ref=scale_out.at[p], dst_ref=scale_in.at[p, plane],
            send_sem=s_send.at[p, o], recv_sem=s_recv.at[p, o],
            device_id={"plane": (plane + o) % 16}, device_id_type=MESH,
        )

    def scale_arrival(p, o):
        src = (plane - o + 16) % 16
        return pltpu.make_async_remote_copy(
            src_ref=scale_in.at[p, src], dst_ref=scale_in.at[p, src],
            send_sem=s_send.at[p, o], recv_sem=s_recv.at[p, o],
            device_id={"plane": src}, device_id_type=MESH,
        )

    def pattern_step(p, _):
        def forward(o):
            x_arrival(p, o).wait_recv()
            core_copy(p, o).start()

        loop(1, 4, forward)
        loop(0, 4, lambda o: core_arrival(p, o).wait_recv())

        def pair_step(t, top):
            b, first = t // 4, t % 4 * 2
            products = []
            for h in range(2):
                orbital = orb[b, first + h].astype(F32)
                v = pot[p, first + h]
                real = v[:, 0].reshape(128, 128).astype(F32)
                imag = v[:, 1].reshape(128, 128).astype(F32)
                products.append(jnp.concatenate([orbital * real, orbital * imag], axis=1))
            high, low = parts(jnp.concatenate(products, axis=0))
            z = dot(high, wz[0]) + (dot(low, wz[0]) + dot(high, wz[1]))
            z = jnp.concatenate(
                [
                    jnp.concatenate([z[:128, :128], z[128:, :128]], axis=1),
                    jnp.concatenate([z[:128, 128:], z[128:, 128:]], axis=1),
                ],
                axis=0,
            )
            high, low = parts(z)
            both = dot(wy[...], high)
            y = both[:64] + (both[64:] + dot(wy[:64], low))
            for h in range(2):
                for j in range(4):
                    cols[pl.ds(b * 32 + j * 8 + first + h, 16, stride=PAD), :] = y[
                        j * 16 : j * 16 + 16, h * 128 : h * 128 + 128
                    ]
            return jnp.maximum(top, jnp.maximum(jnp.abs(y[:, :128]), jnp.abs(y[:, 128:])))

        top = lax.fori_loop(0, 8, pair_step, jnp.zeros((64, 128), F32))
        top = jnp.max(jnp.max(top, axis=0, keepdims=True), axis=1, keepdims=True)
        scale = jnp.maximum(top, 1e-30) * (1.0 / RANGE)
        inverse = 1.0 / scale
        scale_out[p] = jnp.broadcast_to(scale, (1, 128))
        scale_in[p, plane] = jnp.broadcast_to(scale, (1, 128))

        def encode_step(d, _):
            block = cols[pl.ds(pl.multiple_of(d * PAD, 8), 64), :]
            sent[p, d] = encode(block, inverse).reshape(8, 8, 128)
            return 0

        lax.fori_loop(0, 16, encode_step, 0)
        loop(1, 16, lambda o: scale_copy(p, o).start())
        loop(1, 16, lambda o: col_copy(p, o).start())
        got[p, plane] = sent[p, plane]
        return 0

    lax.fori_loop(0, n_pat, pattern_step, 0)

    lane = lax.broadcasted_iota(jnp.int32, (64, 128), 1)

    def finish(p, _):
        loop(1, 16, lambda o: scale_arrival(p, o).wait_recv())
        loop(1, 16, lambda o: col_arrival(p, o).wait_recv())
        scales = scale_in[p]

        def band_step(b, _):
            blocks = []
            for j in range(4):
                blocks.append(decode(got[p, :, b * 4 + j], scales).reshape(128, 128))
            high, low = parts(jnp.concatenate(blocks, axis=1))
            both = dot(wx[...], high)
            x = both[:128] + (both[128:] + dot(wx[:128], low))
            for j in range(4):
                cosine = x[:64, j * 128 : j * 128 + 128]
                sine = pltpu.roll(x[64:, j * 128 : j * 128 + 128], 64, 1)
                value = cosine + jnp.where(lane < 64, -sine, sine)
                kinetic = kinetic_coef * (kx2[...] + ky2[j] + kz2[...])
                value = value * (1.0 / (1.0 + kinetic / energy[b]))
                out[pl.ds((b * 4 + p) * 256 + j, 64, stride=4), :] = value
            return 0

        lax.fori_loop(0, 2, band_step, 0)
        return 0

    lax.fori_loop(0, n_pat, finish, 0)

    loop(1, 32, lambda o: chunk_copy(o).wait_send())

    def drain(p, _):
        loop(1, 4, lambda o: y_copy(p, o).wait_send())
        loop(1, 4, lambda o: x_copy(p, o).wait_send())
        loop(0, 4, lambda o: core_copy(p, o).wait_send())
        loop(1, 16, lambda o: scale_copy(p, o).wait_send())
        loop(1, 16, lambda o: col_copy(p, o).wait_send())
        return 0

    lax.fori_loop(0, n_pat, drain, 0)


def per_device(orbitals, potential_slots, pattern_owner, retained, band_energy):
    length = orbitals.shape[2]
    cz, sz = make_table(retained[2], length)
    wz = jnp.concatenate(
        [
            jnp.concatenate([cz, sz, -sz, cz], axis=1),
            jnp.concatenate([-sz, cz, -cz, -sz], axis=1),
        ],
        axis=0,
    )
    wz = jnp.stack(split(wz))
    cy, sy = make_table(retained[1].reshape(16, 4).T.reshape(64), length)
    wy = jnp.concatenate(split(jnp.concatenate([cy.T, sy.T], axis=1)), axis=0)
    cx, sx = make_table(retained[0], length)
    wx = jnp.concatenate(split(jnp.concatenate([cx.T, sx.T], axis=0)), axis=0)
    ky = lax.dynamic_slice_in_dim(retained[1], lax.axis_index("plane") * 4, 4)
    ky2 = signed_square(ky, length)
    kx2 = jnp.broadcast_to(signed_square(retained[0], length)[:, None], (64, 128))
    kz2 = jnp.tile(signed_square(retained[2], length), 2)[None, :]
    smem = pl.BlockSpec(memory_space=pltpu.SMEM)
    vmem = pl.BlockSpec(memory_space=pltpu.VMEM)
    dma = pltpu.SemaphoreType.DMA
    out = pl.pallas_call(
        kernel,
        out_shape=jax.ShapeDtypeStruct((2048, 128), F32),
        in_specs=[smem] * 3 + [vmem] * 7,
        out_specs=vmem,
        scratch_shapes=[
            pltpu.VMEM((32, 2, 32, 128), BF16),
            pltpu.VMEM((4, 8, 4, 2, 32, 128), BF16),
            pltpu.VMEM((16 * PAD, 128), F32),
            pltpu.VMEM((4, 16, 8, 8, 128), BF16),
            pltpu.VMEM((4, 16, 8, 8, 128), BF16),
            pltpu.VMEM((4, 1, 128), F32),
            pltpu.VMEM((4, 16, 1, 128), F32),
            dma((32,)), dma((32,)),
            dma((4, 4)), dma((4, 4)), dma((4, 4)), dma((4, 4)), dma((4, 4)), dma((4, 4)),
            dma((4, 16)), dma((4, 16)), dma((4, 16)), dma((4, 16)),
        ],
        compiler_params=pltpu.CompilerParams(
            collective_id=0, has_side_effects=True, vmem_limit_bytes=48 * 1024 * 1024
        ),
    )(
        pattern_owner, band_energy, ky2, orbitals, potential_slots[0],
        wz, wy, wx, kx2, kz2,
    )
    return out.reshape(2, 4, 64, 4, 128)


def solution(mesh):
    in_specs = (
        P("band", "plane", None, None),
        P("band", None, "plane", None, None),
        P(),
        P(),
        P("band"),
    )
    out_specs = P("band", None, None, "plane", None)
    return jax.shard_map(
        per_device, mesh=mesh, in_specs=in_specs, out_specs=out_specs, check_vma=False
    )
```

time: 422 us -> 85.1 us (0.20)
  waiting for transfers between devices: 331 us -> 0 us
  Pallas kernels: 0 us -> 79.7 us
  starting transfers between devices: 39.8 us -> 0 us
  matrix products: 16.4 us -> 0 us
  between operations: 16.2 us -> 0.12 us
  other arithmetic: 8.69 us -> 1.08 us
  local copies, waits for them, and re-layouts: 8.1 us -> 3.18 us
    psum x1 -> x0, waiting for transfers between devices: 293 us -> none  [broadcast(): return lax.psum(block, axis)]
    pallas_call x0 -> x1, Pallas kernels: none -> 79.7 us  [per_device(): pl.pallas_call(kernel, out_shape=jax.ShapeDtypeStruct((2048, 128), F32),...]
    all_to_all x4 -> x0, starting transfers between devices: 39.8 us -> none  [per_device(): lax.all_to_all(planes, 'plane', split_axis=3, concat_axis=2, tiled=True)]
    all_to_all x4 -> x0, waiting for transfers between devices: 38.2 us -> none  [per_device(): lax.all_to_all(planes, 'plane', split_axis=3, concat_axis=2, tiled=True)]
    dot_general x12 -> x0, matrix products: 16.4 us -> none  [the longest x4 8.63 us: per_device(): jnp.dot(product.reshape(-1, length), table_z, precision=highest)]
    broadcast_in_dim x4 -> x1, local copies, waits for them, and re-layouts: 4.43 us -> 0.07 us  [per_device(): jnp.broadcast_to(signed_square(retained[0], length)[:, None], (64, 128))]
  transfers between devices with their start and end apart: 5 -> 0, of which waited for: 5 -> 0; matrix products, arithmetic and copies ran while one was open for 5% -> 0% of each run, Pallas kernels for 0% -> 0%
where the time goes in v1:
time: 85.1 us; the launch traced here: 84.1 us
  Pallas kernels  79.7 us (94%)
  local copies, waits for them, and re-layouts  3.18 us (4%)
  other arithmetic  1.08 us (1%)
    pallas_call x1, Pallas kernels, per_device(): pl.pallas_call(kernel, out_shape=jax.ShapeDtypeStruct((2048, 128), F32),...  79.7 us
    unnamed x11, local copies, waits for them, and re-layouts  2.75 us

profile of v1, /device:TPU:1, one launch (start us, length us, event | category | flops | bytes accessed | tf_op | source)
XLA Modules:
  0.0 84.1 jit_solution(167178142428105086)
XLA Ops:
  0.0 0.0 copy-start.4
  0.0 0.7 copy-done.4
  0.7 0.1 broadcast_in_dim_tile.3.kz2
  0.8 0.1 fusion.24.ky2
  0.9 0.1 reshape_squeeze.3
  1.0 0.1 copy.7
  1.0 0.1 mul.111
  1.1 0.1 broadcast_in_dim.2.kx2
  1.2 0.2 cosine_multiply_fusion.2
  1.5 0.2 cosine_multiply_fusion.1
  1.7 0.3 negate_multiply_fusion
  2.0 0.2 maximum_bitcast_fusion
  2.2 0.0 copy-start
  2.2 0.0 copy-start.1
  2.3 0.0 copy-start.2
  2.3 0.0 copy-start.3
  2.3 0.9 %copy-done = bf16[2,8,128,128]{3,2,1,0:T(8,128)(2,1)S(1)} copy-done((bf16[2,8,128,128]{3,2,1,0:T(8,128)(2,1)S(1)}, bf16[2,8,128,128]{3,2,1,0:T(8,128)(2,1)}, u32[]{:S(2)}) %copy-start) | copy-done | bytes 524312
  3.2 0.2 copy-done.1
  3.4 0.0 copy-done.2
  3.4 0.0 copy-done.3
  3.4 79.7 %shard_map.55 = f32[2048,128]{1,0:T(8,128)S(1)} custom-call(s32[4]{0:T(128)S(1)} %copy-done.2, f32[2]{0:T(128)S(1)} %copy-done.3, f32[4]{0:T(128)S(1)} %fusion.24.ky2, bf16[2,8,128,128]{3,2,1,0:T(8,128)(2,1)S(1)} %copy-done, bf16[2,8,128,128]{3,2,1,0:T(8,128)(2,1)S(1)} %bitcast.18, bf16[2,256,256]{2,1,0:T(8,128)(2,1)S(1)} %pad_maximum_fusion.1.wz, ...), custom_call_target="tpu_custom_call" | custom-call | tf_op jit(solution)/shard_map/pallas_call | solution.py:322
  83.2 1.0 %copy.9 = f32[2,4,64,4,128]{4,3,2,1,0:T(4,128)} copy(f32[2,4,64,4,128]{4,3,2,1,0:T(4,128)S(1)} %bitcast.17) | data formatting | bytes 2097152
  (10 shorter events, 0.1 us)
Async XLA Ops:
  0.0 0.7 copy-start.4
  2.2 1.0 %copy-start = (bf16[2,8,128,128]{3,2,1,0:T(8,128)(2,1)S(1)}, bf16[2,8,128,128]{3,2,1,0:T(8,128)(2,1)}, u32[]{:S(2)}) copy-start(bf16[2,8,128,128]{3,2,1,0:T(8,128)(2,1)} %orb.1) | copy-start | bytes 1572868
  2.2 1.2 %copy-start.1 = (bf16[1,2,8,128,128]{4,3,2,1,0:T(8,128)(2,1)S(1)}, bf16[1,2,8,128,128]{4,3,2,1,0:T(8,128)(2,1)}, u32[]{:S(2)}) copy-start(bf16[1,2,8,128,128]{4,3,2,1,0:T(8,128)(2,1)} %param.6) | copy-start | bytes 1572868
  2.3 1.1 %copy-start.2 = (s32[4]{0:T(128)S(1)}, s32[4]{0:T(128)}, u32[]{:S(2)}) copy-start(s32[4]{0:T(128)} %owner.1) | copy-start | bytes 52
  2.3 1.1 %copy-start.3 = (f32[2]{0:T(128)S(1)}, f32[2]{0:T(128)}, u32[]{:S(2)}) copy-start(f32[2]{0:T(128)} %energy.1) | copy-start | bytes 28

commit v2 on v0

v2 whole, which is shorter than its diff:
```python
import functools
import math

import jax
import jax.numpy as jnp
from jax import lax
from jax.experimental import pallas as pl
from jax.experimental.pallas import tpu as pltpu
from jax.sharding import PartitionSpec as P

kinetic_coef = 0.5 * (2.0 * math.pi / 64.0) ** 2
MESH = pl.DeviceIdType.MESH
F32 = jnp.float32
BF16 = jnp.bfloat16
PAD = 72
POWER = 17.5
RANGE = 8192.0
SHIFT = 125.0 * math.log(2.0)


def table(phase):
    angles = (phase & 127).astype(F32) * (2.0 * math.pi / 128)
    return jnp.cos(angles) * (1.0 / math.sqrt(128))


def signed_square(frequency):
    signed = jnp.where(frequency < 64, frequency, frequency - 128).astype(F32)
    return signed * signed


def iota(shape, dimension):
    return lax.broadcasted_iota(jnp.int32, shape, dimension)


def encode(value, inverse_scale):
    u = jnp.abs(value) * inverse_scale
    w = u + jnp.sqrt(u * u + 1.0)
    code = jnp.exp(POWER * jnp.log(w) - SHIFT)
    return jnp.where(value < 0.0, -code, code).astype(BF16)


def decode(code, scale):
    code = code.astype(F32)
    w = jnp.exp((jnp.log(jnp.abs(code)) + SHIFT) * (1.0 / POWER))
    u = (0.5 * scale) * (w - 1.0 / w)
    return jnp.where(code < 0.0, -u, u)


def parts(value):
    high = value.astype(BF16)
    return high, (value - high.astype(F32)).astype(BF16)


def dot(a, b):
    return jnp.dot(a, b, preferred_element_type=F32)


def loop(low, high, step):
    def body(o, _):
        step(o)
        return 0

    lax.fori_loop(low, high, body, 0)


def kernel(
    owner, energy, kept_scalar, kept, orb_hbm, slot_hbm, out,
    orb, slot, wz, wy, wx, precond,
    chunks, picked, pot, cols, sent, got, scale_out, scale_in, plain,
    load, a_send, a_recv, b_send, b_recv, y_send, y_recv, x_send, x_recv, c_send, c_recv,
    d_send, d_recv, s_send, s_recv,
):
    band, plane = lax.axis_index("band"), lax.axis_index("plane")
    row, spot = band // 8, band % 8
    half, upper = row // 2, row % 2
    member = band % 16
    col, core = spot // 2, spot % 2

    def remote(src, dst, send_sem, recv_sem, **to):
        return pltpu.make_async_remote_copy(
            src_ref=src, dst_ref=dst, send_sem=send_sem, recv_sem=recv_sem,
            device_id=to, device_id_type=MESH,
        )

    load_slot = pltpu.make_async_copy(slot_hbm.at[0], slot, load.at[0])
    load_orb = pltpu.make_async_copy(orb_hbm, orb, load.at[1])
    load_slot.start()
    load_orb.start()

    barrier = pltpu.get_barrier_semaphore()

    def greet(**to):
        pl.semaphore_signal(barrier, 1, device_id=to, device_id_type=MESH)

    loop(1, 16, lambda o: greet(band=half * 16 + (member + o) % 16))
    greet(band=(band + 16) % 32)
    loop(1, 16, lambda o: greet(plane=(plane + o) % 16))
    pl.semaphore_wait(barrier, 31)
    load_slot.wait()

    def chunk_of(h, to_spot, to_upper):
        rows = pl.multiple_of(to_spot % 4 * 32 + to_upper * 16, 16)
        return slot.at[:, 2 * h + to_spot // 4, pl.ds(rows, 16), :]

    def chunk_copy(h, o):
        peer = (member + o) % 16
        return remote(
            chunk_of(h, peer % 8, peer // 8), chunks.at[h, member],
            a_send.at[h, o], a_recv.at[h, o], band=half * 16 + peer,
        )

    def chunk_arrival(h, o):
        src = (member - o + 16) % 16
        return remote(
            chunks.at[h, src], chunks.at[h, src],
            a_send.at[h, o], a_recv.at[h, o], band=half * 16 + src,
        )

    def half_copy(h):
        return remote(
            picked.at[h, 0], picked.at[h, 1], b_send.at[h], b_recv.at[h], band=(band + 16) % 32
        )

    def half_arrival(h):
        return remote(
            picked.at[h, 1], picked.at[h, 1], b_send.at[h], b_recv.at[h], band=(band + 16) % 32
        )

    def neighbour():
        return half * 16 + (1 - upper) * 8 + spot

    def y_copy(h):
        return remote(
            pot.at[h, spot, upper], pot.at[h, spot, upper],
            y_send.at[h], y_recv.at[h], band=neighbour(),
        )

    def y_arrival(h):
        return remote(
            pot.at[h, spot, 1 - upper], pot.at[h, spot, 1 - upper],
            y_send.at[h], y_recv.at[h], band=neighbour(),
        )

    def x_copy(h, o):
        return remote(
            pot.at[h, spot], pot.at[h, spot], x_send.at[h, o], x_recv.at[h, o],
            band=row * 8 + (col + o) % 4 * 2 + core,
        )

    def x_arrival(h, o):
        src = (col - o + 4) % 4 * 2 + core
        return remote(
            pot.at[h, src], pot.at[h, src], x_send.at[h, o], x_recv.at[h, o], band=row * 8 + src
        )

    def core_copy(h, o):
        src = (col - o + 4) % 4 * 2 + core
        return remote(
            pot.at[h, src], pot.at[h, src], c_send.at[h, o], c_recv.at[h, o],
            band=row * 8 + col * 2 + 1 - core,
        )

    def core_arrival(h, o):
        src = (col - o + 4) % 4 * 2 + 1 - core
        return remote(
            pot.at[h, src], pot.at[h, src], c_send.at[h, o], c_recv.at[h, o],
            band=row * 8 + col * 2 + 1 - core,
        )

    def col_copy(h, o):
        peer = (plane + o) % 16
        return remote(
            sent.at[h, peer], got.at[h, plane], d_send.at[h, o], d_recv.at[h, o], plane=peer
        )

    def col_arrival(h, o):
        src = (plane - o + 16) % 16
        return remote(
            got.at[h, src], got.at[h, src], d_send.at[h, o], d_recv.at[h, o], plane=src
        )

    def scale_copy(h, o):
        return remote(
            scale_out.at[h], scale_in.at[h, plane], s_send.at[h, o], s_recv.at[h, o],
            plane=(plane + o) % 16,
        )

    def scale_arrival(h, o):
        src = (plane - o + 16) % 16
        return remote(
            scale_in.at[h, src], scale_in.at[h, src], s_send.at[h, o], s_recv.at[h, o], plane=src
        )

    def send_chunks(h):
        loop(1, 16, lambda o: chunk_copy(h, o).start())
        rows = pl.multiple_of(spot % 4 * 32 + upper * 16, 16)
        chunks[h, member] = slot[:, 2 * h + spot // 4, pl.ds(rows, 16), :]

    send_chunks(0)
    send_chunks(1)

    lane4 = iota((1, 256), 1) // 64
    shift_top = jnp.where(lane4 == 1, 32, jnp.where(lane4 == 2, 96, 0))
    shift_low = jnp.where(lane4 == 1, 0, jnp.where(lane4 == 2, 64, 96))
    position = iota((256, 256), 0)
    freq_z = jnp.concatenate([kept[2:3, :]] * 4, axis=1)
    phase = (position & 127) * freq_z + jnp.where(position < 128, shift_top, shift_low)
    high, low = parts(table(phase))
    wz[0] = high
    wz[1] = low
    quarter = jnp.where(iota((1, 128), 1) < 64, 0, 32)
    position = iota((128, 128), 0)
    freq_y = jnp.concatenate([kept[1:2, :]] * 2, axis=1)
    cols[0:128, :] = table(position * freq_y + quarter).T
    for j in range(4):
        for k in range(2):
            high, low = parts(cols[pl.ds(k * 64 + j, 16, stride=4), :])
            wy[j * 16 : j * 16 + 16, k * 128 : k * 128 + 128] = high
            wy[64 + j * 16 : 80 + j * 16, k * 128 : k * 128 + 128] = low
    freq_x = jnp.concatenate([kept[0:1, :]] * 2, axis=1)
    position = position // 2 % 16 * 8 + position // 32 * 2 + position % 2
    high, low = parts(table(position * freq_x + quarter).T)
    wx[:128] = high
    wx[128:] = low
    kx2 = jnp.broadcast_to(signed_square(freq_x), (128, 128)).T[:64]
    kz2 = signed_square(jnp.concatenate([kept[2:3, :]] * 2, axis=1))
    for j in range(4):
        ky2 = signed_square(kept_scalar[1, plane * 4 + j])
        kinetic = kinetic_coef * (kx2 + ky2 + kz2)
        for b in range(2):
            precond[b * 4 + j] = 1.0 / (1.0 + kinetic / energy[b])
    load_orb.wait()

    def pick(h):
        loop(1, 16, lambda o: chunk_arrival(h, o).wait_recv())
        wanted = [owner[p] % 16 for p in range(4)]
        found = [chunks[h, 0]] * 4
        for m in range(1, 16):
            chunk = chunks[h, m]
            found = [jnp.where(wanted[p] == m, chunk, found[p]) for p in range(4)]
        for p in range(4):
            picked[h, 0, p] = found[p]
        half_copy(h).start()

    def settle(h):
        half_arrival(h).wait_recv()
        for p in range(4):
            inside = owner[p] // 16 == half
            pot[h, spot, upper, p] = jnp.where(inside, picked[h, 0, p], picked[h, 1, p])
        y_copy(h).start()

    def spread(h):
        y_arrival(h).wait_recv()
        loop(1, 4, lambda o: x_copy(h, o).start())
        core_copy(h, 0).start()

    def forward(h):
        def step(o):
            x_arrival(h, o).wait_recv()
            core_copy(h, o).start()

        loop(1, 4, step)

    def transform(h):
        loop(0, 4, lambda o: core_arrival(h, o).wait_recv())

        def band_step(b, top):
            products = []
            for p in range(4):
                for k in range(2):
                    orbital = orb[b, 2 * h + k].astype(F32)
                    real = pot[h, k * 4 : k * 4 + 4, :, p, 0].reshape(128, 128).astype(F32)
                    imag = pot[h, k * 4 : k * 4 + 4, :, p, 1].reshape(128, 128).astype(F32)
                    products.append(jnp.concatenate([orbital * real, orbital * imag], axis=1))
            high, low = parts(jnp.concatenate(products, axis=0))
            z = dot(high, wz[0]) + (dot(low, wz[0]) + dot(high, wz[1]))
            for p in range(4):
                even = z[p * 256 : p * 256 + 128]
                odd = z[p * 256 + 128 : p * 256 + 256]
                pair = jnp.concatenate(
                    [
                        jnp.concatenate([even[:, :128], odd[:, :128]], axis=1),
                        jnp.concatenate([even[:, 128:], odd[:, 128:]], axis=1),
                    ],
                    axis=0,
                )
                high, low = parts(pair)
                both = dot(wy[...], high)
                y = both[:64] + (both[64:] + dot(wy[:64], low))
                for k in range(2):
                    for j in range(4):
                        cols[pl.ds(b * 32 + p * 8 + k * 4 + j, 16, stride=PAD), :] = y[
                            j * 16 : j * 16 + 16, k * 128 : k * 128 + 128
                        ]
                top = jnp.maximum(top, jnp.maximum(jnp.abs(y[:, :128]), jnp.abs(y[:, 128:])))
            return top

        top = lax.fori_loop(0, 2, band_step, jnp.zeros((64, 128), F32))
        top = jnp.max(jnp.max(top, axis=0, keepdims=True), axis=1, keepdims=True)
        scale = jnp.maximum(top, 1e-30) * (1.0 / RANGE)
        inverse = 1.0 / scale
        scale_out[h] = jnp.broadcast_to(scale, (1, 128))
        scale_in[h, plane] = jnp.broadcast_to(scale, (1, 128))

        def encode_step(d, _):
            block = cols[pl.ds(pl.multiple_of(d * PAD, 8), 64), :]
            sent[h, d] = encode(block, inverse).reshape(8, 8, 128)
            return 0

        lax.fori_loop(0, 16, encode_step, 0, unroll=4)
        loop(1, 16, lambda o: scale_copy(h, o).start())
        loop(1, 16, lambda o: col_copy(h, o).start())
        got[h, plane] = sent[h, plane]

    def stage(t, _):
        @pl.when(t >= 4)
        def _():
            transform(t - 4)

        @pl.when((t >= 3) & (t < 7))
        def _():
            forward(t - 3)

        @pl.when((t >= 2) & (t < 6))
        def _():
            spread(t - 2)

        @pl.when((t >= 1) & (t < 5))
        def _():
            settle(t - 1)

        @pl.when(t < 4)
        def _():
            pick(t)

        @pl.when(t < 2)
        def _():
            send_chunks(t + 2)

        return 0

    lax.fori_loop(0, 8, stage, 0)

    def receive(h, _):
        loop(1, 16, lambda o: scale_arrival(h, o).wait_recv())
        loop(1, 16, lambda o: col_arrival(h, o).wait_recv())
        scales = scale_in[h]
        for n in range(8):
            rows = pl.multiple_of(n * 512 + h * 128, 128)
            plain[pl.ds(rows, 128), :] = decode(got[h, :, n], scales).reshape(128, 128)
        return 0

    lax.fori_loop(0, 4, receive, 0)

    lane = iota((64, 128), 1)

    def finish(n, _):
        blocks = [plain[pl.ds(n * 512 + j, 128, stride=4), :] for j in range(4)]
        high, low = parts(jnp.concatenate(blocks, axis=1))
        both = dot(wx[...], high)
        x = both[:128] + (both[128:] + dot(wx[:128], low))
        for j in range(4):
            cosine = x[:64, j * 128 : j * 128 + 128]
            sine = pltpu.roll(x[64:, j * 128 : j * 128 + 128], 64, 1)
            value = cosine + jnp.where(lane < 64, -sine, sine)
            out[pl.ds(n * 256 + j, 64, stride=4), :] = value * precond[n // 4 * 4 + j]
        return 0

    lax.fori_loop(0, 8, finish, 0, unroll=2)

    def drain(h, _):
        loop(1, 16, lambda o: chunk_copy(h, o).wait_send())
        half_copy(h).wait_send()
        y_copy(h).wait_send()
        loop(1, 4, lambda o: x_copy(h, o).wait_send())
        loop(0, 4, lambda o: core_copy(h, o).wait_send())
        loop(1, 16, lambda o: scale_copy(h, o).wait_send())
        loop(1, 16, lambda o: col_copy(h, o).wait_send())
        return 0

    lax.fori_loop(0, 4, drain, 0)


def per_device(orbitals, potential_slots, pattern_owner, retained, band_energy):
    smem = pl.BlockSpec(memory_space=pltpu.SMEM)
    vmem = pl.BlockSpec(memory_space=pltpu.VMEM)
    dma = pltpu.SemaphoreType.DMA
    out = pl.pallas_call(
        kernel,
        out_shape=jax.ShapeDtypeStruct((2048, 128), F32),
        in_specs=[smem] * 3 + [vmem] + [pl.BlockSpec(memory_space=pl.ANY)] * 2,
        out_specs=vmem,
        scratch_shapes=[
            pltpu.VMEM((2, 8, 128, 128), BF16),
            pltpu.VMEM((2, 8, 128, 128), BF16),
            pltpu.VMEM((2, 256, 256), BF16),
            pltpu.VMEM((128, 256), BF16),
            pltpu.VMEM((256, 128), BF16),
            pltpu.VMEM((8, 64, 128), F32),
            pltpu.VMEM((4, 16, 2, 16, 128), BF16),
            pltpu.VMEM((4, 2, 4, 2, 16, 128), BF16),
            pltpu.VMEM((4, 8, 2, 4, 2, 16, 128), BF16),
            pltpu.VMEM((16 * PAD, 128), F32),
            pltpu.VMEM((4, 16, 8, 8, 128), BF16),
            pltpu.VMEM((4, 16, 8, 8, 128), BF16),
            pltpu.VMEM((4, 1, 128), F32),
            pltpu.VMEM((4, 16, 1, 128), F32),
            pltpu.VMEM((4096, 128), F32),
            dma((2,)), dma((4, 16)), dma((4, 16)), dma((4,)), dma((4,)), dma((4,)), dma((4,)),
            dma((4, 4)), dma((4, 4)), dma((4, 4)), dma((4, 4)),
            dma((4, 16)), dma((4, 16)), dma((4, 16)), dma((4, 16)),
        ],
        compiler_params=pltpu.CompilerParams(
            collective_id=0, has_side_effects=True, vmem_limit_bytes=60 * 1024 * 1024
        ),
    )(pattern_owner, band_energy, retained, retained, orbitals, potential_slots)
    return out.reshape(2, 4, 64, 4, 128)


def solution(mesh):
    in_specs = (
        P("band", "plane", None, None),
        P("band", None, "plane", None, None),
        P(),
        P(),
        P("band"),
    )
    out_specs = P("band", None, None, "plane", None)
    return jax.shard_map(
        per_device, mesh=mesh, in_specs=in_specs, out_specs=out_specs, check_vma=False
    )
```

time: 422 us -> 77.7 us (0.18)
  waiting for transfers between devices: 331 us -> 0 us
  Pallas kernels: 0 us -> 75.3 us
  starting transfers between devices: 39.8 us -> 0 us
  matrix products: 16.4 us -> 0 us
  between operations: 16.2 us -> 0.01 us
  other arithmetic: 8.69 us -> 0 us
  local copies, waits for them, and re-layouts: 8.1 us -> 2.27 us
    psum x1 -> x0, waiting for transfers between devices: 293 us -> none  [broadcast(): return lax.psum(block, axis)]
    pallas_call x0 -> x1, Pallas kernels: none -> 75.3 us  [per_device(): pl.pallas_call(kernel, out_shape=jax.ShapeDtypeStruct((2048, 128), F32),...]
    all_to_all x4 -> x0, starting transfers between devices: 39.8 us -> none  [per_device(): lax.all_to_all(planes, 'plane', split_axis=3, concat_axis=2, tiled=True)]
    all_to_all x4 -> x0, waiting for transfers between devices: 38.2 us -> none  [per_device(): lax.all_to_all(planes, 'plane', split_axis=3, concat_axis=2, tiled=True)]
    dot_general x12 -> x0, matrix products: 16.4 us -> none  [the longest x4 8.63 us: per_device(): jnp.dot(product.reshape(-1, length), table_z, precision=highest)]
    broadcast_in_dim x4 -> x0, local copies, waits for them, and re-layouts: 4.43 us -> none  [per_device(): jnp.concatenate([along_y[:, :, :kept_count, :kept_count] - along_y[:, :,...]
  transfers between devices with their start and end apart: 5 -> 0, of which waited for: 5 -> 0; matrix products, arithmetic and copies ran while one was open for 5% -> 0% of each run, Pallas kernels for 0% -> 0%
where the time goes in v2:
time: 77.7 us; the launch traced here: 77.5 us
  Pallas kernels  75.3 us (97%)
  local copies, waits for them, and re-layouts  2.27 us (3%)
    pallas_call x1, Pallas kernels, per_device(): pl.pallas_call(kernel, out_shape=jax.ShapeDtypeStruct((2048, 128), F32),...  75.3 us
    unnamed x1, local copies, waits for them, and re-layouts  2.27 us

profile of v2, /device:TPU:1, one launch (start us, length us, event | category | flops | bytes accessed | tf_op | source)
XLA Modules:
  0.0 77.5 jit_solution(1674346816602252523)
XLA Ops:
  0.0 75.3 %shard_map.55 = f32[2048,128]{1,0:T(8,128)} custom-call(s32[4]{0:T(128)} %owner.1, f32[2]{0:T(128)} %energy.1, s32[3,64]{1,0:T(4,128)} %kept.1, s32[3,64]{1,0:T(4,128)} %kept.1, bf16[2,8,128,128]{3,2,1,0:T(8,128)(2,1)} %orb_hbm.1, bf16[1,2,8,128,128]{4,3,2,1,0:T(8,128)(2,1)} %slot_hbm.1), custom_call_target="tpu_custom_call" | custom-call | tf_op jit(solution)/shard_map/pallas_call | solution.py:388
  75.3 2.3 %copy.7 = f32[2,4,64,4,128]{4,3,2,1,0:T(4,128)} copy(f32[2,4,64,4,128]{4,3,2,1,0:T(4,128)} %bitcast.1) | data formatting | bytes 2097152

commit v3 on v2

--- a/solution.py
+++ b/solution.py
@@ -13,14 +13,20 @@
 F32 = jnp.float32
 BF16 = jnp.bfloat16
 PAD = 72
+UNR = True
 POWER = 17.5
 RANGE = 8192.0
 SHIFT = 125.0 * math.log(2.0)
 
 
 def table(phase):
-    angles = (phase & 127).astype(F32) * (2.0 * math.pi / 128)
-    return jnp.cos(angles) * (1.0 / math.sqrt(128))
+    half = (((phase + 64) & 127) - 64).astype(F32) * (math.pi / 128)
+    square = half * half
+    series = jnp.full_like(half, 1.0 / math.factorial(13))
+    for n in (11, 9, 7, 5, 3, 1):
+        series = (1.0 if n % 4 == 1 else -1.0) / math.factorial(n) + series * square
+    sine = half * series
+    return (1.0 - 2.0 * sine * sine) * (1.0 / math.sqrt(128))
 
 
 def signed_square(frequency):
@@ -60,13 +66,13 @@
         step(o)
         return 0
 
-    lax.fori_loop(low, high, body, 0)
+    lax.fori_loop(low, high, body, 0, unroll=UNR)
 
 
 def kernel(
     owner, energy, kept_scalar, kept, orb_hbm, slot_hbm, out,
     orb, slot, wz, wy, wx, precond,
-    chunks, picked, pot, cols, sent, got, scale_out, scale_in, plain,
+    chunks, picked, pot, cols, sent, got, scale_out, scale_in, plain, partial,
     load, a_send, a_recv, b_send, b_recv, y_send, y_recv, x_send, x_recv, c_send, c_recv,
     d_send, d_recv, s_send, s_recv,
 ):
@@ -217,18 +223,6 @@
             high, low = parts(cols[pl.ds(k * 64 + j, 16, stride=4), :])
             wy[j * 16 : j * 16 + 16, k * 128 : k * 128 + 128] = high
             wy[64 + j * 16 : 80 + j * 16, k * 128 : k * 128 + 128] = low
-    freq_x = jnp.concatenate([kept[0:1, :]] * 2, axis=1)
-    position = position // 2 % 16 * 8 + position // 32 * 2 + position % 2
-    high, low = parts(table(position * freq_x + quarter).T)
-    wx[:128] = high
-    wx[128:] = low
-    kx2 = jnp.broadcast_to(signed_square(freq_x), (128, 128)).T[:64]
-    kz2 = signed_square(jnp.concatenate([kept[2:3, :]] * 2, axis=1))
-    for j in range(4):
-        ky2 = signed_square(kept_scalar[1, plane * 4 + j])
-        kinetic = kinetic_coef * (kx2 + ky2 + kz2)
-        for b in range(2):
-            precond[b * 4 + j] = 1.0 / (1.0 + kinetic / energy[b])
     load_orb.wait()
 
     def pick(h):
@@ -341,24 +335,42 @@
 
     lax.fori_loop(0, 8, stage, 0)
 
-    def receive(h, _):
+    freq_x = jnp.concatenate([kept[0:1, :]] * 2, axis=1)
+    position = position // 2 % 16 * 8 + position // 32 * 2 + position % 2
+    high, low = parts(table(position * freq_x + quarter).T)
+    wx[:128] = high
+    wx[128:] = low
+    kx2 = jnp.broadcast_to(signed_square(freq_x), (128, 128)).T[:64]
+    kz2 = signed_square(jnp.concatenate([kept[2:3, :]] * 2, axis=1))
+    for j in range(4):
+        ky2 = signed_square(kept_scalar[1, plane * 4 + j])
+        kinetic = kinetic_coef * (kx2 + ky2 + kz2)
+        for b in range(2):
+            precond[b * 4 + j] = 1.0 / (1.0 + kinetic / energy[b])
+
+    def receive(h):
         loop(1, 16, lambda o: scale_arrival(h, o).wait_recv())
         loop(1, 16, lambda o: col_arrival(h, o).wait_recv())
         scales = scale_in[h]
         for n in range(8):
             rows = pl.multiple_of(n * 512 + h * 128, 128)
             plain[pl.ds(rows, 128), :] = decode(got[h, :, n], scales).reshape(128, 128)
+
+    def x_sum(n, first, count):
+        blocks = [plain[pl.ds(n * 512 + first * 128 + j, 32 * count, stride=4), :] for j in range(4)]
+        high, low = parts(jnp.concatenate(blocks, axis=1))
+        keys = slice(first * 32, (first + count) * 32)
+        both = dot(wx[:, keys], high)
+        return both[:128] + (both[128:] + dot(wx[:128, keys], low))
+
+    lane = iota((64, 128), 1)
+
+    def begin(n, _):
+        partial[n] = x_sum(n, 0, 3)
         return 0
 
-    lax.fori_loop(0, 4, receive, 0)
-
-    lane = iota((64, 128), 1)
-
     def finish(n, _):
-        blocks = [plain[pl.ds(n * 512 + j, 128, stride=4), :] for j in range(4)]
-        high, low = parts(jnp.concatenate(blocks, axis=1))
-        both = dot(wx[...], high)
-        x = both[:128] + (both[128:] + dot(wx[:128], low))
+        x = partial[n] + x_sum(n, 3, 1)
         for j in range(4):
             cosine = x[:64, j * 128 : j * 128 + 128]
             sine = pltpu.roll(x[64:, j * 128 : j * 128 + 128], 64, 1)
@@ -366,6 +378,9 @@
             out[pl.ds(n * 256 + j, 64, stride=4), :] = value * precond[n // 4 * 4 + j]
         return 0
 
+    lax.fori_loop(0, 3, lambda h, c: (receive(h), c)[1], 0)
+    lax.fori_loop(0, 8, begin, 0, unroll=2)
+    receive(3)
     lax.fori_loop(0, 8, finish, 0, unroll=2)
 
     def drain(h, _):
@@ -387,8 +402,8 @@
     dma = pltpu.SemaphoreType.DMA
     out = pl.pallas_call(
         kernel,
-        out_shape=jax.ShapeDtypeStruct((2048, 128), F32),
-        in_specs=[smem] * 3 + [vmem] + [pl.BlockSpec(memory_space=pl.ANY)] * 2,
+        out_shape=pltpu.VMEM((2048, 128), F32),
+        in_specs=[smem] * 3 + [vmem] + [pl.BlockSpec(memory_space=pltpu.HBM)] * 2,
         out_specs=vmem,
         scratch_shapes=[
             pltpu.VMEM((2, 8, 128, 128), BF16),
@@ -406,14 +421,19 @@
             pltpu.VMEM((4, 1, 128), F32),
             pltpu.VMEM((4, 16, 1, 128), F32),
             pltpu.VMEM((4096, 128), F32),
+            pltpu.VMEM((8, 128, 512), F32),
             dma((2,)), dma((4, 16)), dma((4, 16)), dma((4,)), dma((4,)), dma((4,)), dma((4,)),
             dma((4, 4)), dma((4, 4)), dma((4, 4)), dma((4, 4)),
             dma((4, 16)), dma((4, 16)), dma((4, 16)), dma((4, 16)),
         ],
         compiler_params=pltpu.CompilerParams(
-            collective_id=0, has_side_effects=True, vmem_limit_bytes=60 * 1024 * 1024
+            collective_id=0, has_side_effects=True, vmem_limit_bytes=65994752
         ),
-    )(pattern_owner, band_energy, retained, retained, orbitals, potential_slots)
+    )(
+        pattern_owner, band_energy, retained, retained,
+        pltpu.with_memory_space_constraint(orbitals, pltpu.HBM),
+        pltpu.with_memory_space_constraint(potential_slots, pltpu.HBM),
+    )
     return out.reshape(2, 4, 64, 4, 128)
 
 

time: 77.7 us -> 73.8 us (0.950)
  Pallas kernels: 75.3 us -> 72.7 us
  local copies, waits for them, and re-layouts: 2.27 us -> 0.97 us
    pallas_call x1, Pallas kernels: 75.3 us -> 72.7 us  [per_device(): pl.pallas_call(kernel, out_shape=pltpu.VMEM((2048, 128), F32), in_specs=[...]
    unnamed x1, local copies, waits for them, and re-layouts: 2.27 us -> 0.97 us
where the time goes in v3:
time: 73.8 us; the launch traced here: 73.7 us
  Pallas kernels  72.7 us (99%)
  local copies, waits for them, and re-layouts  0.97 us (1%)
    pallas_call x1, Pallas kernels, per_device(): pl.pallas_call(kernel, out_shape=pltpu.VMEM((2048, 128), F32), in_specs=[...  72.7 us

profile of v3, /device:TPU:1, one launch (start us, length us, event | category | flops | bytes accessed | tf_op | source)
XLA Modules:
  0.0 73.7 jit_solution(15990143439379741667)
XLA Ops:
  0.0 72.7 %shard_map.55 = f32[2048,128]{1,0:T(8,128)S(1)} custom-call(s32[4]{0:T(128)} %owner.1, f32[2]{0:T(128)} %energy.1, s32[3,64]{1,0:T(4,128)} %kept.1, s32[3,64]{1,0:T(4,128)} %kept.1, bf16[2,8,128,128]{3,2,1,0:T(8,128)(2,1)} %orb_hbm.1, bf16[1,2,8,128,128]{4,3,2,1,0:T(8,128)(2,1)} %slot_hbm.1), custom_call_target="tpu_custom_call" | custom-call | tf_op jit(solution)/shard_map/pallas_call | solution.py:403
  72.7 1.0 %copy.7 = f32[2,4,64,4,128]{4,3,2,1,0:T(4,128)} copy(f32[2,4,64,4,128]{4,3,2,1,0:T(4,128)S(1)} %bitcast.1) | data formatting | bytes 2097152

commit v4 on v3

--- a/solution.py
+++ b/solution.py
@@ -74,7 +74,7 @@
     orb, slot, wz, wy, wx, precond,
     chunks, picked, pot, cols, sent, got, scale_out, scale_in, plain, partial,
     load, a_send, a_recv, b_send, b_recv, y_send, y_recv, x_send, x_recv, c_send, c_recv,
-    d_send, d_recv, s_send, s_recv,
+    d_send, d_recv, s_send, s_recv, rounds,
 ):
     band, plane = lax.axis_index("band"), lax.axis_index("plane")
     row, spot = band // 8, band % 8
@@ -95,13 +95,19 @@
 
     barrier = pltpu.get_barrier_semaphore()
 
-    def greet(**to):
-        pl.semaphore_signal(barrier, 1, device_id=to, device_id_type=MESH)
-
-    loop(1, 16, lambda o: greet(band=half * 16 + (member + o) % 16))
-    greet(band=(band + 16) % 32)
-    loop(1, 16, lambda o: greet(plane=(plane + o) % 16))
-    pl.semaphore_wait(barrier, 31)
+    def greet(semaphore, **to):
+        pl.semaphore_signal(semaphore, 1, device_id=to, device_id_type=MESH)
+
+    def greet_along_z(semaphore, distance):
+        for step in (distance, 8 - distance):
+            greet(semaphore, plane=plane // 8 * 8 + (plane + step) % 8)
+
+    greet(barrier, plane=(plane + 8) % 16)
+    loop(1, 16, lambda o: greet(barrier, band=half * 16 + (member + o) % 16))
+    greet(barrier, band=(band + 16) % 32)
+    greet_along_z(barrier, 1)
+    pl.semaphore_wait(barrier, 19)
+    greet_along_z(rounds.at[0], 1)
     load_slot.wait()
 
     def chunk_of(h, to_spot, to_upper):
@@ -306,34 +312,23 @@
         loop(1, 16, lambda o: col_copy(h, o).start())
         got[h, plane] = sent[h, plane]
 
-    def stage(t, _):
-        @pl.when(t >= 4)
-        def _():
+    for t in range(8):
+        if t >= 4:
             transform(t - 4)
-
-        @pl.when((t >= 3) & (t < 7))
-        def _():
+        if 3 <= t < 7:
             forward(t - 3)
-
-        @pl.when((t >= 2) & (t < 6))
-        def _():
+        if 2 <= t < 6:
             spread(t - 2)
-
-        @pl.when((t >= 1) & (t < 5))
-        def _():
+        if 1 <= t < 5:
             settle(t - 1)
-
-        @pl.when(t < 4)
-        def _():
+        if t < 4:
             pick(t)
-
-        @pl.when(t < 2)
-        def _():
+        if t < 2:
             send_chunks(t + 2)
-
-        return 0
-
-    lax.fori_loop(0, 8, stage, 0)
+        if t < 3:
+            pl.semaphore_wait(rounds.at[t], 2)
+        if t < 2:
+            greet_along_z(rounds.at[t + 1], 2 - t)
 
     freq_x = jnp.concatenate([kept[0:1, :]] * 2, axis=1)
     position = position // 2 % 16 * 8 + position // 32 * 2 + position % 2
@@ -378,7 +373,8 @@
             out[pl.ds(n * 256 + j, 64, stride=4), :] = value * precond[n // 4 * 4 + j]
         return 0
 
-    lax.fori_loop(0, 3, lambda h, c: (receive(h), c)[1], 0)
+    for h in range(3):
+        receive(h)
     lax.fori_loop(0, 8, begin, 0, unroll=2)
     receive(3)
     lax.fori_loop(0, 8, finish, 0, unroll=2)
@@ -425,6 +421,7 @@
             dma((2,)), dma((4, 16)), dma((4, 16)), dma((4,)), dma((4,)), dma((4,)), dma((4,)),
             dma((4, 4)), dma((4, 4)), dma((4, 4)), dma((4, 4)),
             dma((4, 16)), dma((4, 16)), dma((4, 16)), dma((4, 16)),
+            pltpu.SemaphoreType.REGULAR((3,)),
         ],
         compiler_params=pltpu.CompilerParams(
             collective_id=0, has_side_effects=True, vmem_limit_bytes=65994752

time: 73.8 us -> 69.5 us (0.942)
  Pallas kernels: 72.7 us -> 67.7 us
    pallas_call x1, Pallas kernels: 72.7 us -> 67.7 us  [per_device(): pl.pallas_call(kernel, out_shape=pltpu.VMEM((2048, 128), F32), in_specs=[...]
where the time goes in v4:
time: 69.5 us; the launch traced here: 68.7 us
  Pallas kernels  67.7 us (97%)
  local copies, waits for them, and re-layouts  0.97 us (1%)
    pallas_call x1, Pallas kernels, per_device(): pl.pallas_call(kernel, out_shape=pltpu.VMEM((2048, 128), F32), in_specs=[...  67.7 us

profile of v4, /device:TPU:1, one launch (start us, length us, event | category | flops | bytes accessed | tf_op | source)
XLA Modules:
  0.0 68.7 jit_solution(16413710848564430546)
XLA Ops:
  0.0 67.7 %shard_map.55 = f32[2048,128]{1,0:T(8,128)S(1)} custom-call(s32[4]{0:T(128)} %owner.1, f32[2]{0:T(128)} %energy.1, s32[3,64]{1,0:T(4,128)} %kept.1, s32[3,64]{1,0:T(4,128)} %kept.1, bf16[2,8,128,128]{3,2,1,0:T(8,128)(2,1)} %orb_hbm.1, bf16[1,2,8,128,128]{4,3,2,1,0:T(8,128)(2,1)} %slot_hbm.1), custom_call_target="tpu_custom_call" | custom-call | tf_op jit(solution)/shard_map/pallas_call | solution.py:399
  67.7 1.0 %copy.7 = f32[2,4,64,4,128]{4,3,2,1,0:T(4,128)} copy(f32[2,4,64,4,128]{4,3,2,1,0:T(4,128)S(1)} %bitcast.1) | data formatting | bytes 2097152

commit v5 on v4

--- a/solution.py
+++ b/solution.py
@@ -308,8 +308,8 @@
             return 0
 
         lax.fori_loop(0, 16, encode_step, 0, unroll=4)
+        loop(1, 16, lambda o: col_copy(h, o).start())
         loop(1, 16, lambda o: scale_copy(h, o).start())
-        loop(1, 16, lambda o: col_copy(h, o).start())
         got[h, plane] = sent[h, plane]
 
     for t in range(8):

time: 69.5 us -> 71.8 us (1.033)
  Pallas kernels: 67.7 us -> 69.9 us
    pallas_call x1, Pallas kernels: 67.7 us -> 69.9 us  [per_device(): pl.pallas_call(kernel, out_shape=pltpu.VMEM((2048, 128), F32), in_specs=[...]
where the time goes in v5:
time: 71.8 us; the launch traced here: 70.8 us
  Pallas kernels  69.9 us (97%)
  local copies, waits for them, and re-layouts  0.97 us (1%)
    pallas_call x1, Pallas kernels, per_device(): pl.pallas_call(kernel, out_shape=pltpu.VMEM((2048, 128), F32), in_specs=[...  69.9 us

profile of v5, /device:TPU:1, one launch (start us, length us, event | category | flops | bytes accessed | tf_op | source)
XLA Modules:
  0.0 70.8 jit_solution(16441374180175349735)
XLA Ops:
  0.0 69.9 %shard_map.55 = f32[2048,128]{1,0:T(8,128)S(1)} custom-call(s32[4]{0:T(128)} %owner.1, f32[2]{0:T(128)} %energy.1, s32[3,64]{1,0:T(4,128)} %kept.1, s32[3,64]{1,0:T(4,128)} %kept.1, bf16[2,8,128,128]{3,2,1,0:T(8,128)(2,1)} %orb_hbm.1, bf16[1,2,8,128,128]{4,3,2,1,0:T(8,128)(2,1)} %slot_hbm.1), custom_call_target="tpu_custom_call" | custom-call | tf_op jit(solution)/shard_map/pallas_call | solution.py:399
  69.9 1.0 %copy.7 = f32[2,4,64,4,128]{4,3,2,1,0:T(4,128)} copy(f32[2,4,64,4,128]{4,3,2,1,0:T(4,128)S(1)} %bitcast.1) | data formatting | bytes 2097152
